TPU v7x, 32 devices: a whole 2x2x4 slice. The times are simulated.
32 devices in a mesh: gx: 2 (over x), gy: 4 (over y, core), ha: 4 (over z).
Axes of the slice: x: 2, y: 2, z: 4, core: 2. Of those that a mesh axis runs over, the one named last changes fastest.
Arguments:
- global_state: float32 [8, 60, 16, 16], P(None, 'ha', 'gx', 'gy'), may hold values from -6 to 6
- crm_state: float32 [8, 60, 16, 1024], P(None, 'ha', 'gx', 'gy'), may hold values from -6 to 6
- mixing: float32 [8, 8], replicated, may hold values from -2 to 2
- substeps: int32 [16, 16], P('gx', 'gy'), may hold values from 1 to 8
- assignment: int32 [16, 16], P('gx', 'gy'), may hold values from 0 to 31, as said below
Outputs:
- new_global: float32 [8, 60, 16, 16], P(None, 'ha', 'gx', 'gy')
- new_crm: float32 [8, 60, 16384], P(None, None, ('gx', 'gy', 'ha'))
Inputs may be any that keep to these rules, and one draw needn't show every extreme that they name: `assignment`: within each tile of 8 x 4 columns every value 0 .. 31 appears once; value // 8 is the helper index, value % 8 the slot on that helper.
All inputs are finite; a program needn't handle non-finite values.
Results may differ from a plain program's by a relative error of at most 0.0003.
Values sent between devices are 32-bit elements; how exact they have to be, the bound alone decides.
A program may use at most 64 MiB of HBM per device.

v0:
```python
import jax
import jax.numpy as jnp
from jax import lax
from jax.sharding import PartitionSpec as P

MAXSUB = 8
GSUB = 4
HIGH = lax.Precision.HIGHEST


def extended(cells, sides, width):
    for axis, dim in sides:
        count = lax.axis_size(axis)
        head = lax.slice_in_dim(cells, 0, width, axis=dim)
        tail = lax.slice_in_dim(cells, cells.shape[dim] - width, cells.shape[dim], axis=dim)
        cells = jnp.concatenate(
            [
                lax.ppermute(tail, axis, [(i, (i + 1) % count) for i in range(count)]),
                cells,
                lax.ppermute(head, axis, [((i + 1) % count, i) for i in range(count)]),
            ],
            axis=dim,
        )
    return cells


def global_operator(padded):
    center = padded[:, :, 1:-1, 1:-1]
    east = padded[:, :, 2:, 1:-1]
    west = padded[:, :, :-2, 1:-1]
    north = padded[:, :, 1:-1, 2:]
    south = padded[:, :, 1:-1, :-2]
    return (
        0.2 * (east + west + north + south - 4.0 * center)
        - 0.15 * (east - west)
        - 0.15 * (north - south)
    )


def crm_update(state, pushed, mixing):
    lateral = jnp.roll(state, 1, axis=3) + jnp.roll(state, -1, axis=3) - 2.0 * state
    upper = jnp.concatenate([state[:, :1], state[:, :-1]], axis=1)
    lower = jnp.concatenate([state[:, 1:], state[:, -1:]], axis=1)
    coupling = jnp.einsum("gf,flsc->glsc", mixing, jnp.tanh(state), precision=HIGH)
    return state + 0.1 * (1.0 * lateral + 0.5 * (upper + lower - 2.0 * state) + pushed + coupling)


def advance(states, pushed, slot_counts, mixing):

    def one_step(index, state):
        updated = crm_update(state, pushed, mixing)
        return jnp.where((index < slot_counts)[:, None], updated, state)

    return lax.fori_loop(0, MAXSUB, one_step, states)


def on_device(global_state, crm_state, mixing, substeps, assignment):
    current = global_state
    for substep in range(GSUB // 2):
        padded = extended(current, (("gx", 2), ("gy", 3)), 2)
        middle = padded[:, :, 1:-1, 1:-1] + 0.5 * global_operator(padded)
        current = middle[:, :, 1:-1, 1:-1] + 0.5 * global_operator(middle)
    forcing = (current - global_state) / (0.5 * GSUB)
    tile_x, tile_y = assignment.shape
    columns = tile_x * tile_y
    helpers = lax.axis_size("ha")
    per_helper = columns // helpers
    fields, level_part = (crm_state.shape[0], crm_state.shape[1])
    width = crm_state.shape[3] // tile_y
    global_fields = forcing.shape[0]
    onehot = (
        assignment.reshape(columns)[:, None] == jnp.arange(columns, dtype=jnp.int32)[None, :]
    ).astype(jnp.float32)
    helper = lax.axis_index("ha")
    own_slots = lax.dynamic_slice_in_dim(onehot, helper * per_helper, per_helper, 1)
    local_states = crm_state.reshape(fields, level_part, columns, width)
    slotted = jnp.einsum("flxc,xj->fljc", local_states, onehot, precision=HIGH)
    pushes = jnp.einsum(
        "glx,xj->glj", forcing.reshape(global_fields, level_part, columns), onehot, precision=HIGH
    )
    pushes = pushes.reshape(global_fields, level_part, columns, 1)
    states, pushed = (
        lax.all_to_all(slotted, "ha", split_axis=2, concat_axis=1, tiled=True),
        lax.all_to_all(pushes, "ha", split_axis=2, concat_axis=1, tiled=True),
    )
    slot_counts = jnp.dot(
        substeps.reshape(1, columns).astype(jnp.float32), own_slots, precision=HIGH
    )
    slot_counts = slot_counts.reshape(per_helper).astype(jnp.int32)
    advanced = advance(states, pushed, slot_counts, mixing)
    tendency = jnp.mean(advanced - states, axis=3)
    returned = lax.all_to_all(tendency, "ha", split_axis=1, concat_axis=2, tiled=True)
    placed = jnp.dot(returned.reshape(fields * level_part, columns), onehot.T, precision=HIGH)
    new_global = current + placed.reshape(fields, level_part, tile_x, tile_y)
    levels_all = advanced.shape[1]
    return (new_global, advanced.reshape(fields, levels_all, per_helper * width))


def solution(mesh):
    in_specs = (
        P(None, "ha", "gx", "gy"),
        P(None, "ha", "gx", "gy"),
        P(),
        P("gx", "gy"),
        P("gx", "gy"),
    )
    out_specs = (P(None, "ha", "gx", "gy"), P(None, None, ("gx", "gy", "ha")))
    return jax.shard_map(
        on_device, mesh=mesh, in_specs=in_specs, out_specs=out_specs, check_vma=False
    )
```

profile of v0, /device:TPU:0, one launch (start us, length us, event | category | flops | bytes accessed | tf_op | source)
XLA Modules:
  0.0 139.4 jit_solution(3381811293322487794)
XLA Ops:
  0.6 0.9 copy.92
  1.6 3.0 %collective-permute-start = (f32[8,15,2,4]{1,2,3,0:T(2,128)S(1)}, f32[8,15,2,4]{1,2,3,0:T(2,128)S(1)}, u32[]{:S(2)}, u32[]{:S(2)}) collective-permute-start(f32[8,15,2,4]{1,2,3,0:T(2,128)S(1)} %get-tuple-element.155), channel_id=1, source_target_pairs={{0,16},{16,0},{1,17},{17,1},{2,18},{18,2},{3,19},{19,3},{4,20},{20... | collective-permute-start | bytes 11528 | tf_op jit(solution)/shard_map/ppermute | solution.py:18
  4.7 1.8 %collective-permute-done = f32[8,15,2,4]{1,2,3,0:T(2,128)S(1)} collective-permute-done((f32[8,15,2,4]{1,2,3,0:T(2,128)S(1)}, f32[8,15,2,4]{1,2,3,0:T(2,128)S(1)}, u32[]{:S(2)}, u32[]{:S(2)}) %collective-permute-start) | collective-permute-done | bytes 3872 | tf_op jit(solution)/shard_map/ppermute | solution.py:18
  6.5 2.0 %collective-permute-done.1 = f32[8,15,2,4]{1,2,3,0:T(2,128)S(1)} collective-permute-done((f32[8,15,2,4]{1,2,3,0:T(2,128)S(1)}, f32[8,15,2,4]{1,2,3,0:T(2,128)S(1)}, u32[]{:S(2)}, u32[]{:S(2)}) %collective-permute-start.1) | collective-permute-done | bytes 3872 | tf_op jit(solution)/shard_map/ppermute | solution.py:20
  8.7 1.7 %collective-permute-start.3 = (f32[8,15,12,2]{1,2,3,0:T(8,128)S(1)}, f32[8,15,12,2]{1,2,3,0:T(8,128)S(1)}, u32[]{:S(2)}, u32[]{:S(2)}) collective-permute-start(f32[8,15,12,2]{1,2,3,0:T(8,128)S(1)} %get-tuple-element.152), channel_id=1, source_target_pairs={{4,0},{8,4},{12,8},{0,12},{5,1},{9,5},{13,9},{1,13},{6,2},{10,6},{... | collective-permute-start | bytes 34568 | tf_op jit(solution)/shard_map/ppermute | solution.py:20
  10.4 2.6 %collective-permute-done.2 = f32[8,15,12,2]{1,2,3,0:T(8,128)S(1)} collective-permute-done((f32[8,15,12,2]{1,2,3,0:T(8,128)S(1)}, f32[8,15,12,2]{1,2,3,0:T(8,128)S(1)}, u32[]{:S(2)}, u32[]{:S(2)}) %collective-permute-start.2) | collective-permute-done | bytes 11552 | tf_op jit(solution)/shard_map/ppermute | solution.py:18
  14.1 0.6 collective-permute-start.4
  14.7 1.5 %collective-permute-start.5 = (f32[8,15,2,4]{1,2,3,0:T(2,128)S(1)}, f32[8,15,2,4]{1,2,3,0:T(2,128)S(1)}, u32[]{:S(2)}, u32[]{:S(2)}) collective-permute-start(f32[8,15,2,4]{1,2,3,0:T(2,128)S(1)} %get-tuple-element.154), channel_id=1, source_target_pairs={{16,0},{0,16},{17,1},{1,17},{18,2},{2,18},{19,3},{3,19},{20,4},{4,... | collective-permute-start | bytes 11528 | tf_op jit(solution)/shard_map/ppermute | solution.py:20
  16.2 2.0 %collective-permute-done.4 = f32[8,15,2,4]{1,2,3,0:T(2,128)S(1)} collective-permute-done((f32[8,15,2,4]{1,2,3,0:T(2,128)S(1)}, f32[8,15,2,4]{1,2,3,0:T(2,128)S(1)}, u32[]{:S(2)}, u32[]{:S(2)}) %collective-permute-start.4) | collective-permute-done | bytes 3872 | tf_op jit(solution)/shard_map/ppermute | solution.py:18
  18.3 0.8 collective-permute-done.5
  19.1 0.7 fusion.29
  19.9 1.6 %collective-permute-start.7 = (f32[8,15,12,2]{1,2,3,0:T(8,128)S(1)}, f32[8,15,12,2]{1,2,3,0:T(8,128)S(1)}, u32[]{:S(2)}, u32[]{:S(2)}) collective-permute-start(f32[8,15,12,2]{1,2,3,0:T(8,128)S(1)} %get-tuple-element.150), channel_id=1, source_target_pairs={{4,0},{8,4},{12,8},{0,12},{5,1},{9,5},{13,9},{1,13},{6,2},{10,6},{... | collective-permute-start | bytes 34568 | tf_op jit(solution)/shard_map/ppermute | solution.py:20
  22.0 2.4 %collective-permute-done.6 = f32[8,15,12,2]{1,2,3,0:T(8,128)S(1)} collective-permute-done((f32[8,15,12,2]{1,2,3,0:T(8,128)}, f32[8,15,12,2]{1,2,3,0:T(8,128)S(1)}, u32[]{:S(2)}, u32[]{:S(2)}) %collective-permute-start.6) | collective-permute-done | bytes 11552 | tf_op jit(solution)/shard_map/ppermute | solution.py:18
  25.9 0.8 reshape.67
  26.7 4.9 %all-to-all-start.1 = ((f32[4,1,960]{2,1,0:T(1,128)}), f32[4,1,960]{2,1,0:T(1,128)S(1)}, u32[]{:S(2)}, u32[]{:S(2)}) async-start(f32[4,1,960]{2,1,0:T(1,128)} %reshape.67), calls=%async_computation.1 | async-start | bytes 32768 | tf_op jit(solution)/shard_map/all_to_all | solution.py:84
  31.5 1.1 convolution_bitcast_fusion
  32.7 1.1 copy.133
  33.9 2.3 %reshape.65 = f32[4,1,61440]{2,1,0:T(1,128)} reshape(f32[32,15,8,64]{3,2,1,0:T(8,128)S(1)} %bitcast.68) | data formatting | bytes 1966080
  36.2 1.0 all-to-all-done.1
  37.2 4.1 %all-to-all-start = ((f32[4,1,61440]{2,1,0:T(1,128)}), f32[4,1,61440]{2,1,0:T(1,128)S(1)}, u32[]{:S(2)}, u32[]{:S(2)}) async-start(f32[4,1,61440]{2,1,0:T(1,128)} %reshape.65), calls=%async_computation | async-start | bytes 1966080 | tf_op jit(solution)/shard_map/all_to_all | solution.py:83
  41.7 0.6 broadcast.101
  42.3 0.7 reduce.1
  43.5 22.7 %all-to-all-done = f32[4,1,61440]{2,1,0:T(1,128)S(1)} async-done(((f32[4,1,61440]{2,1,0:T(1,128)}), f32[4,1,61440]{2,1,0:T(1,128)S(1)}, u32[]{:S(2)}, u32[]{:S(2)}) %all-to-all-start) | async-done | bytes 983072 | tf_op jit(solution)/shard_map/all_to_all | solution.py:83
  66.2 3.5 %reduce = f32[4,61440]{1,0:T(4,128)S(1)} reduce(f32[4,1,61440]{2,1,0:T(1,128)S(1)} %all-to-all-done, f32[]{:T(128)} %broadcast.101), dimensions={1}, to_apply=%all_to_all.37.reduce_sub_computation | reduce | bytes 1966084 | tf_op jit(solution)/shard_map/all_to_all | solution.py:83
  69.7 1.0 reshape.66
  71.1 1.1 copy-done
  72.2 53.0 %while.13 = (s32[]{:T(128)}, f32[8,60,8,64]{3,0,2,1:T(8,128)S(1)}, s32[8]{0:T(128)S(1)}, f32[8,60,8,1]{0,2,1,3:T(8,128)S(1)}, f32[8,8]{1,0:T(8,128)S(1)}, /*index=5*/s32[]{:T(128)}) while((s32[]{:T(128)}, f32[8,60,8,64]{3,0,2,1:T(8,128)S(1)}, s32[8]{0:T(128)S(1)}, f32[8,60,8,1]{0,2,1,3:T(8,128)S(1)}, f32[8,8]{1,0:T(8,128)S(1)}, ...), condition=%wide.region_1.2_spmd, body=%wide.region_0.1_spmd.sunk | while | flops 27525128 | bytes 15744385 | solution.py:54
  72.4 0.5 fusion.45
  72.9 0.8 fusion.44
  73.7 0.8 fusion.43
  74.4 4.4 %add_select_fusion.2 = f32[8,60,8,64]{3,0,2,1:T(8,128)S(1)} fusion(f32[8,60,8,64]{3,0,2,1:T(8,128)S(1)} %copy.145, f32[8,60,8,63]{3,0,2,1:T(8,128)S(1)} %get-tuple-element.196, f32[8,60,8,1]{3,0,2,1:T(8,128)S(1)} %get-tuple-element.197, f32[8,60,8,1]{3,0,2,1:T(8,128)S(1)} %get-tuple-element.198, f32[8,60,8,63]{3,0,2,1:T(8,128)S(1)} %get-tuple-element.199, ...), kind=kOutput, calls=%fused_computation.clone.1 | convolution fusion | flops 27525120 | bytes 5913864 | tf_op jit(solution)/shard_map/while/body/eval_jaxpr/gf,flsc->glsc/dot_general | solution.py:44
  79.0 0.5 fusion.45
  79.5 0.8 fusion.44
  80.3 0.8 fusion.43
  81.1 4.4 %add_select_fusion.2 = f32[8,60,8,64]{3,0,2,1:T(8,128)S(1)} fusion(f32[8,60,8,64]{3,0,2,1:T(8,128)S(1)} %copy.145, f32[8,60,8,63]{3,0,2,1:T(8,128)S(1)} %get-tuple-element.196, f32[8,60,8,1]{3,0,2,1:T(8,128)S(1)} %get-tuple-element.197, f32[8,60,8,1]{3,0,2,1:T(8,128)S(1)} %get-tuple-element.198, f32[8,60,8,63]{3,0,2,1:T(8,128)S(1)} %get-tuple-element.199, ...), kind=kOutput, calls=%fused_computation.clone.1 | convolution fusion | flops 27525120 | bytes 5913864 | tf_op jit(solution)/shard_map/while/body/eval_jaxpr/gf,flsc->glsc/dot_general | solution.py:44
  85.6 0.5 fusion.45
  86.2 0.8 fusion.44
  86.9 0.8 fusion.43
  87.7 4.4 %add_select_fusion.2 = f32[8,60,8,64]{3,0,2,1:T(8,128)S(1)} fusion(f32[8,60,8,64]{3,0,2,1:T(8,128)S(1)} %copy.145, f32[8,60,8,63]{3,0,2,1:T(8,128)S(1)} %get-tuple-element.196, f32[8,60,8,1]{3,0,2,1:T(8,128)S(1)} %get-tuple-element.197, f32[8,60,8,1]{3,0,2,1:T(8,128)S(1)} %get-tuple-element.198, f32[8,60,8,63]{3,0,2,1:T(8,128)S(1)} %get-tuple-element.199, ...), kind=kOutput, calls=%fused_computation.clone.1 | convolution fusion | flops 27525120 | bytes 5913864 | tf_op jit(solution)/shard_map/while/body/eval_jaxpr/gf,flsc->glsc/dot_general | solution.py:44
  92.8 0.8 fusion.44
  93.5 0.8 fusion.43
  94.3 4.4 %add_select_fusion.2 = f32[8,60,8,64]{3,0,2,1:T(8,128)S(1)} fusion(f32[8,60,8,64]{3,0,2,1:T(8,128)S(1)} %copy.145, f32[8,60,8,63]{3,0,2,1:T(8,128)S(1)} %get-tuple-element.196, f32[8,60,8,1]{3,0,2,1:T(8,128)S(1)} %get-tuple-element.197, f32[8,60,8,1]{3,0,2,1:T(8,128)S(1)} %get-tuple-element.198, f32[8,60,8,63]{3,0,2,1:T(8,128)S(1)} %get-tuple-element.199, ...), kind=kOutput, calls=%fused_computation.clone.1 | convolution fusion | flops 27525120 | bytes 5913864 | tf_op jit(solution)/shard_map/while/body/eval_jaxpr/gf,flsc->glsc/dot_general | solution.py:44
  98.9 0.5 fusion.45
  99.4 0.8 fusion.44
  100.2 0.8 fusion.43
  101.0 4.4 %add_select_fusion.2 = f32[8,60,8,64]{3,0,2,1:T(8,128)S(1)} fusion(f32[8,60,8,64]{3,0,2,1:T(8,128)S(1)} %copy.145, f32[8,60,8,63]{3,0,2,1:T(8,128)S(1)} %get-tuple-element.196, f32[8,60,8,1]{3,0,2,1:T(8,128)S(1)} %get-tuple-element.197, f32[8,60,8,1]{3,0,2,1:T(8,128)S(1)} %get-tuple-element.198, f32[8,60,8,63]{3,0,2,1:T(8,128)S(1)} %get-tuple-element.199, ...), kind=kOutput, calls=%fused_computation.clone.1 | convolution fusion | flops 27525120 | bytes 5913864 | tf_op jit(solution)/shard_map/while/body/eval_jaxpr/gf,flsc->glsc/dot_general | solution.py:44
  106.0 0.8 fusion.44
  106.8 0.8 fusion.43
  107.6 4.4 %add_select_fusion.2 = f32[8,60,8,64]{3,0,2,1:T(8,128)S(1)} fusion(f32[8,60,8,64]{3,0,2,1:T(8,128)S(1)} %copy.145, f32[8,60,8,63]{3,0,2,1:T(8,128)S(1)} %get-tuple-element.196, f32[8,60,8,1]{3,0,2,1:T(8,128)S(1)} %get-tuple-element.197, f32[8,60,8,1]{3,0,2,1:T(8,128)S(1)} %get-tuple-element.198, f32[8,60,8,63]{3,0,2,1:T(8,128)S(1)} %get-tuple-element.199, ...), kind=kOutput, calls=%fused_computation.clone.1 | convolution fusion | flops 27525120 | bytes 5913864 | tf_op jit(solution)/shard_map/while/body/eval_jaxpr/gf,flsc->glsc/dot_general | solution.py:44
  112.2 0.5 fusion.45
  112.7 0.8 fusion.44
  113.4 0.8 fusion.43
  114.2 4.4 %add_select_fusion.2 = f32[8,60,8,64]{3,0,2,1:T(8,128)S(1)} fusion(f32[8,60,8,64]{3,0,2,1:T(8,128)S(1)} %copy.145, f32[8,60,8,63]{3,0,2,1:T(8,128)S(1)} %get-tuple-element.196, f32[8,60,8,1]{3,0,2,1:T(8,128)S(1)} %get-tuple-element.197, f32[8,60,8,1]{3,0,2,1:T(8,128)S(1)} %get-tuple-element.198, f32[8,60,8,63]{3,0,2,1:T(8,128)S(1)} %get-tuple-element.199, ...), kind=kOutput, calls=%fused_computation.clone.1 | convolution fusion | flops 27525120 | bytes 5913864 | tf_op jit(solution)/shard_map/while/body/eval_jaxpr/gf,flsc->glsc/dot_general | solution.py:44
  119.3 0.8 fusion.44
  120.1 0.8 fusion.43
  120.8 4.4 %add_select_fusion.2 = f32[8,60,8,64]{3,0,2,1:T(8,128)S(1)} fusion(f32[8,60,8,64]{3,0,2,1:T(8,128)S(1)} %copy.145, f32[8,60,8,63]{3,0,2,1:T(8,128)S(1)} %get-tuple-element.196, f32[8,60,8,1]{3,0,2,1:T(8,128)S(1)} %get-tuple-element.197, f32[8,60,8,1]{3,0,2,1:T(8,128)S(1)} %get-tuple-element.198, f32[8,60,8,63]{3,0,2,1:T(8,128)S(1)} %get-tuple-element.199, ...), kind=kOutput, calls=%fused_computation.clone.1 | convolution fusion | flops 27525120 | bytes 5913864 | tf_op jit(solution)/shard_map/while/body/eval_jaxpr/gf,flsc->glsc/dot_general | solution.py:44
  125.2 2.1 %subtract_reduce_fusion = f32[8,60,8]{0,2,1:T(8,128)S(1)} fusion(f32[8,60,8,64]{3,0,2,1:T(8,128)S(1)} %get-tuple-element.96, f32[8,60,8,64]{3,0,2,1:T(8,128)} %bitcast.65), kind=kLoop, calls=%fused_computation.14 | loop fusion | flops 487680 | bytes 1981440 | tf_op jit(solution)/shard_map/reduce_sum | solution.py:91
  127.7 0.8 reshape.69
  128.5 3.3 %all-to-all-start.2 = ((f32[4,1,960]{2,1,0:T(1,128)}), f32[4,1,960]{2,1,0:T(1,128)S(1)}, u32[]{:S(2)}, u32[]{:S(2)}) async-start(f32[4,1,960]{2,1,0:T(1,128)} %reshape.69), calls=%async_computation.2 | async-start | bytes 32768 | tf_op jit(solution)/shard_map/all_to_all | solution.py:92
  131.8 1.7 %copy.112 = f32[8,60,8,64]{3,2,0,1:T(8,128)} copy(f32[8,60,8,64]{3,0,2,1:T(8,128)S(1)} %get-tuple-element.96) | data formatting | bytes 1966080 | tf_op jit(solution)/shard_map/while | solution.py:54
  133.5 2.6 %reshape.56 = f32[8,60,512]{2,0,1:T(8,128)} reshape(f32[8,60,8,64]{3,2,0,1:T(8,128)} %copy.112) | data formatting | bytes 1966080 | tf_op jit(solution)/shard_map/reshape | solution.py:96
  136.1 1.2 all-to-all-done.2
  137.4 0.7 reduce.2
  138.7 0.7 copy.113
  (76 shorter events, 8.4 us)
Async XLA Ops:
  1.6 4.9 %collective-permute-start = (f32[8,15,2,4]{1,2,3,0:T(2,128)S(1)}, f32[8,15,2,4]{1,2,3,0:T(2,128)S(1)}, u32[]{:S(2)}, u32[]{:S(2)}) collective-permute-start(f32[8,15,2,4]{1,2,3,0:T(2,128)S(1)} %get-tuple-element.155), channel_id=1, source_target_pairs={{0,16},{16,0},{1,17},{17,1},{2,18},{18,2},{3,19},{19,3},{4,20},{20... | collective-permute-start | bytes 11528 | tf_op jit(solution)/shard_map/ppermute | solution.py:18
  4.6 3.9 %collective-permute-start.1 = (f32[8,15,2,4]{1,2,3,0:T(2,128)S(1)}, f32[8,15,2,4]{1,2,3,0:T(2,128)S(1)}, u32[]{:S(2)}, u32[]{:S(2)}) collective-permute-start(f32[8,15,2,4]{1,2,3,0:T(2,128)S(1)} %get-tuple-element.156), channel_id=1, source_target_pairs={{16,0},{0,16},{17,1},{1,17},{18,2},{2,18},{19,3},{3,19},{20,4},{4,... | collective-permute-start | bytes 11528 | tf_op jit(solution)/shard_map/ppermute | solution.py:20
  8.6 4.4 %collective-permute-start.2 = (f32[8,15,12,2]{1,2,3,0:T(8,128)S(1)}, f32[8,15,12,2]{1,2,3,0:T(8,128)S(1)}, u32[]{:S(2)}, u32[]{:S(2)}) collective-permute-start(f32[8,15,12,2]{1,2,3,0:T(8,128)S(1)} %get-tuple-element.151), channel_id=1, source_target_pairs={{0,4},{4,8},{8,12},{12,0},{1,5},{5,9},{9,13},{13,1},{2,6},{6,10},{... | collective-permute-start | bytes 34568 | tf_op jit(solution)/shard_map/ppermute | solution.py:18
  8.7 4.8 %collective-permute-start.3 = (f32[8,15,12,2]{1,2,3,0:T(8,128)S(1)}, f32[8,15,12,2]{1,2,3,0:T(8,128)S(1)}, u32[]{:S(2)}, u32[]{:S(2)}) collective-permute-start(f32[8,15,12,2]{1,2,3,0:T(8,128)S(1)} %get-tuple-element.152), channel_id=1, source_target_pairs={{4,0},{8,4},{12,8},{0,12},{5,1},{9,5},{13,9},{1,13},{6,2},{10,6},{... | collective-permute-start | bytes 34568 | tf_op jit(solution)/shard_map/ppermute | solution.py:20
  13.6 7.9 %copy-start.4 = (s32[8,4]{0,1:T(4,128)S(1)}, s32[8,4]{0,1:T(4,128)}, u32[]{:S(2)}) copy-start(s32[8,4]{0,1:T(4,128)} %param.11) | copy-start | bytes 388
  13.6 8.1 %copy-start.1 = (f32[8,15,8,256]{3,2,1,0:T(8,128)S(1)}, f32[8,15,8,256]{3,2,1,0:T(8,128)}, u32[]{:S(2)}) copy-start(f32[8,15,8,256]{3,2,1,0:T(8,128)} %param.8) | copy-start | bytes 2949124
  14.1 4.1 %collective-permute-start.4 = (f32[8,15,2,4]{1,2,3,0:T(2,128)S(1)}, f32[8,15,2,4]{1,2,3,0:T(2,128)S(1)}, u32[]{:S(2)}, u32[]{:S(2)}) collective-permute-start(f32[8,15,2,4]{1,2,3,0:T(2,128)S(1)} %get-tuple-element.153), channel_id=1, source_target_pairs={{0,16},{16,0},{1,17},{17,1},{2,18},{18,2},{3,19},{19,3},{4,20},{20... | collective-permute-start | bytes 11528 | tf_op jit(solution)/shard_map/ppermute | solution.py:18
  14.7 4.3 %collective-permute-start.5 = (f32[8,15,2,4]{1,2,3,0:T(2,128)S(1)}, f32[8,15,2,4]{1,2,3,0:T(2,128)S(1)}, u32[]{:S(2)}, u32[]{:S(2)}) collective-permute-start(f32[8,15,2,4]{1,2,3,0:T(2,128)S(1)} %get-tuple-element.154), channel_id=1, source_target_pairs={{16,0},{0,16},{17,1},{1,17},{18,2},{2,18},{19,3},{3,19},{20,4},{4,... | collective-permute-start | bytes 11528 | tf_op jit(solution)/shard_map/ppermute | solution.py:20
  19.7 4.6 %collective-permute-start.6 = (f32[8,15,12,2]{1,2,3,0:T(8,128)}, f32[8,15,12,2]{1,2,3,0:T(8,128)S(1)}, u32[]{:S(2)}, u32[]{:S(2)}) collective-permute-start(f32[8,15,12,2]{1,2,3,0:T(8,128)} %get-tuple-element.149), channel_id=1, source_target_pairs={{0,4},{4,8},{8,12},{12,0},{1,5},{5,9},{9,13},{13,1},{2,6},{6,10},{... | collective-permute-start | bytes 34568 | tf_op jit(solution)/shard_map/ppermute | solution.py:18
  19.9 4.9 %collective-permute-start.7 = (f32[8,15,12,2]{1,2,3,0:T(8,128)S(1)}, f32[8,15,12,2]{1,2,3,0:T(8,128)S(1)}, u32[]{:S(2)}, u32[]{:S(2)}) collective-permute-start(f32[8,15,12,2]{1,2,3,0:T(8,128)S(1)} %get-tuple-element.150), channel_id=1, source_target_pairs={{4,0},{8,4},{12,8},{0,12},{5,1},{9,5},{13,9},{1,13},{6,2},{10,6},{... | collective-permute-start | bytes 34568 | tf_op jit(solution)/shard_map/ppermute | solution.py:20
  22.0 3.3 %copy-start.2 = (f32[8,15,8,4]{1,3,2,0:T(4,128)S(1)}, f32[8,15,8,4]{1,3,2,0:T(4,128)}, u32[]{:S(2)}) copy-start(f32[8,15,8,4]{1,3,2,0:T(4,128)} %param.7) | copy-start | bytes 46084
  26.7 10.5 %all-to-all-start.1 = ((f32[4,1,960]{2,1,0:T(1,128)}), f32[4,1,960]{2,1,0:T(1,128)S(1)}, u32[]{:S(2)}, u32[]{:S(2)}) async-start(f32[4,1,960]{2,1,0:T(1,128)} %reshape.67), calls=%async_computation.1 | async-start | bytes 32768 | tf_op jit(solution)/shard_map/all_to_all | solution.py:84
  33.9 7.4 %copy-start.5 = (s32[8,4]{0,1:T(4,128)S(1)}, s32[8,4]{0,1:T(4,128)}, u32[]{:S(2)}) copy-start(s32[8,4]{0,1:T(4,128)} %param.10) | copy-start | bytes 388
  37.2 29.0 %all-to-all-start = ((f32[4,1,61440]{2,1,0:T(1,128)}), f32[4,1,61440]{2,1,0:T(1,128)S(1)}, u32[]{:S(2)}, u32[]{:S(2)}) async-start(f32[4,1,61440]{2,1,0:T(1,128)} %reshape.65), calls=%async_computation | async-start | bytes 1966080 | tf_op jit(solution)/shard_map/all_to_all | solution.py:83
  70.9 1.3 copy-start
  70.9 1.3 copy-start.3
  128.5 8.8 %all-to-all-start.2 = ((f32[4,1,960]{2,1,0:T(1,128)}), f32[4,1,960]{2,1,0:T(1,128)S(1)}, u32[]{:S(2)}, u32[]{:S(2)}) async-start(f32[4,1,960]{2,1,0:T(1,128)} %reshape.69), calls=%async_computation.2 | async-start | bytes 32768 | tf_op jit(solution)/shard_map/all_to_all | solution.py:92
where the time goes:
time: 140 us; the launch traced here: 139 us
  waiting for transfers between devices  37.3 us (27%)
  matrix products  37 us (26%)
  local copies, waits for them, and re-layouts  34.2 us (24%)
  starting transfers between devices  21 us (15%)
  other arithmetic  8.49 us (6%)
    dot_general x8, matrix products, crm_update(): jnp.einsum('gf,flsc->glsc', mixing, jnp.tanh(state), precision=HIGH)  35.1 us
    all_to_all x1, waiting for transfers between devices, on_device(): lax.all_to_all(slotted, 'ha', split_axis=2, concat_axis=1, tiled=True)  22.7 us
    slice x16, local copies, waits for them, and re-layouts, crm_update(): jnp.roll(state, -1, axis=3)  12.2 us
    ppermute x4, waiting for transfers between devices, extended(): lax.ppermute(tail, axis, [(i, (i + 1) % count) for i in range(count)])  8.83 us
    unnamed x22, local copies, waits for them, and re-layouts  8.09 us
    ppermute x4, starting transfers between devices, extended(): lax.ppermute(head, axis, [((i + 1) % count, i) for i in range(count)])  4.93 us
    all_to_all x1, starting transfers between devices, on_device(): lax.all_to_all(pushes, 'ha', split_axis=2, concat_axis=1, tiled=True)  4.86 us
    all_to_all x1, starting transfers between devices, on_device(): lax.all_to_all(slotted, 'ha', split_axis=2, concat_axis=1, tiled=True)  4.12 us
  transfers between devices with their start and end apart: 11, of which 11 were waited for; matrix products, arithmetic and copies ran while one was open for 8% of the time, Pallas kernels for 0%

commit v1 on v0

--- a/solution.py
+++ b/solution.py
@@ -1,11 +1,22 @@
+import functools
 import jax
 import jax.numpy as jnp
 from jax import lax
 from jax.sharding import PartitionSpec as P
+from jax.lax import all_to_all, axis_size
 
 MAXSUB = 8
 GSUB = 4
 HIGH = lax.Precision.HIGHEST
+
+
+def play_tokens(buf, a_name):
+    return jnp.concatenate(
+        all_to_all(jnp.stack(jnp.split(buf, axis_size(a_name), 2)), a_name, 0, 0), 1
+    )
+
+
+slot_deliver = functools.partial(play_tokens, a_name="ha")
 
 
 def extended(cells, sides, width):
@@ -80,7 +91,7 @@
     )
     pushes = pushes.reshape(global_fields, level_part, columns, 1)
     states, pushed = (
-        lax.all_to_all(slotted, "ha", split_axis=2, concat_axis=1, tiled=True),
+        slot_deliver(slotted),
         lax.all_to_all(pushes, "ha", split_axis=2, concat_axis=1, tiled=True),
     )
     slot_counts = jnp.dot(

time: 140 us -> 140 us (level)
  waiting for transfers between devices: 37.3 us -> 35.5 us
  other arithmetic: 8.49 us -> 10.2 us
    ppermute x4, waiting for transfers between devices: 8.83 us -> 6.3 us  [extended(): lax.ppermute(tail, axis, [(i, (i + 1) % count) for i in range(count)])]
    while x2 -> x3, local copies, waits for them, and re-layouts: 2.02 us -> 3.16 us  [advance(): return lax.fori_loop(0, MAXSUB, one_step, states)]
    unnamed x22 -> x23, local copies, waits for them, and re-layouts: 8.09 us -> 7.67 us
  transfers between devices with their start and end apart: 11 -> 11, of which waited for: 11 -> 11; matrix products, arithmetic and copies ran while one was open for 8% -> 10% of each run, Pallas kernels for 0% -> 0%
where the time goes in v1:
time: 140 us; the launch traced here: 139 us
  matrix products  37.1 us (26%)
  waiting for transfers between devices  35.5 us (25%)
  local copies, waits for them, and re-layouts  34.5 us (25%)
  starting transfers between devices  20.4 us (15%)
  other arithmetic  10.2 us (7%)
    dot_general x8, matrix products, crm_update(): jnp.einsum('gf,flsc->glsc', mixing, jnp.tanh(state), precision=HIGH)  35.2 us
    all_to_all x1, waiting for transfers between devices, play_tokens(): all_to_all(jnp.stack(jnp.split(buf, axis_size(a_name), 2)), a_name, 0, 0)  22.2 us
    slice x16, local copies, waits for them, and re-layouts, crm_update(): jnp.roll(state, -1, axis=3)  12.2 us
    unnamed x23, local copies, waits for them, and re-layouts  7.67 us
    ppermute x4, waiting for transfers between devices, extended(): lax.ppermute(tail, axis, [(i, (i + 1) % count) for i in range(count)])  6.3 us
    ppermute x4, starting transfers between devices, extended(): lax.ppermute(head, axis, [((i + 1) % count, i) for i in range(count)])  4.94 us
    all_to_all x1, starting transfers between devices, on_device(): lax.all_to_all(pushes, 'ha', split_axis=2, concat_axis=1, tiled=True)  4.69 us
    slice x16, local copies, waits for them, and re-layouts, crm_update(): lower = jnp.concatenate([state[:, 1:], state[:, -1:]], axis=1)  4.03 us
  transfers between devices with their start and end apart: 11, of which 11 were waited for; matrix products, arithmetic and copies ran while one was open for 10% of the time, Pallas kernels for 0%

profile of v1, /device:TPU:0, one launch (start us, length us, event | category | flops | bytes accessed | tf_op | source)
XLA Modules:
  0.0 139.1 jit_solution(1636751220639650904)
XLA Ops:
  0.6 1.0 copy.75
  1.7 3.0 %collective-permute-start = (f32[8,15,2,4]{1,2,3,0:T(2,128)S(1)}, f32[8,15,2,4]{1,2,3,0:T(2,128)S(1)}, u32[]{:S(2)}, u32[]{:S(2)}) collective-permute-start(f32[8,15,2,4]{1,2,3,0:T(2,128)S(1)} %get-tuple-element.157), channel_id=1, source_target_pairs={{0,16},{16,0},{1,17},{17,1},{2,18},{18,2},{3,19},{19,3},{4,20},{20... | collective-permute-start | bytes 11528 | tf_op jit(solution)/shard_map/ppermute | solution.py:29
  4.8 1.8 %collective-permute-done = f32[8,15,2,4]{1,2,3,0:T(2,128)S(1)} collective-permute-done((f32[8,15,2,4]{1,2,3,0:T(2,128)S(1)}, f32[8,15,2,4]{1,2,3,0:T(2,128)S(1)}, u32[]{:S(2)}, u32[]{:S(2)}) %collective-permute-start) | collective-permute-done | bytes 3872 | tf_op jit(solution)/shard_map/ppermute | solution.py:29
  6.6 2.0 %collective-permute-done.1 = f32[8,15,2,4]{1,2,3,0:T(2,128)S(1)} collective-permute-done((f32[8,15,2,4]{1,2,3,0:T(2,128)S(1)}, f32[8,15,2,4]{1,2,3,0:T(2,128)S(1)}, u32[]{:S(2)}, u32[]{:S(2)}) %collective-permute-start.1) | collective-permute-done | bytes 3872 | tf_op jit(solution)/shard_map/ppermute | solution.py:31
  8.7 0.7 fusion.31
  9.4 1.7 %collective-permute-start.3 = (f32[8,15,12,2]{1,2,3,0:T(8,128)S(1)}, f32[8,15,12,2]{1,2,3,0:T(8,128)S(1)}, u32[]{:S(2)}, u32[]{:S(2)}) collective-permute-start(f32[8,15,12,2]{1,2,3,0:T(8,128)S(1)} %get-tuple-element.154), channel_id=1, source_target_pairs={{4,0},{8,4},{12,8},{0,12},{5,1},{9,5},{13,9},{1,13},{6,2},{10,6},{... | collective-permute-start | bytes 34568 | tf_op jit(solution)/shard_map/ppermute | solution.py:31
  11.1 0.8 copy.78
  12.3 1.7 %collective-permute-done.2 = f32[8,15,12,2]{1,2,3,0:T(8,128)S(1)} collective-permute-done((f32[8,15,12,2]{1,2,3,0:T(8,128)}, f32[8,15,12,2]{1,2,3,0:T(8,128)S(1)}, u32[]{:S(2)}, u32[]{:S(2)}) %collective-permute-start.2) | collective-permute-done | bytes 11552 | tf_op jit(solution)/shard_map/ppermute | solution.py:29
  15.0 0.6 collective-permute-start.4
  15.6 1.5 %collective-permute-start.5 = (f32[8,15,2,4]{1,2,3,0:T(2,128)S(1)}, f32[8,15,2,4]{1,2,3,0:T(2,128)S(1)}, u32[]{:S(2)}, u32[]{:S(2)}) collective-permute-start(f32[8,15,2,4]{1,2,3,0:T(2,128)S(1)} %get-tuple-element.156), channel_id=1, source_target_pairs={{16,0},{0,16},{17,1},{1,17},{18,2},{2,18},{19,3},{3,19},{20,4},{4,... | collective-permute-start | bytes 11528 | tf_op jit(solution)/shard_map/ppermute | solution.py:31
  17.1 1.1 convolution_bitcast_fusion
  18.3 1.1 collective-permute-done.4
  19.3 0.7 collective-permute-done.5
  20.3 1.6 %collective-permute-start.7 = (f32[8,15,12,2]{1,2,3,0:T(8,128)S(1)}, f32[8,15,12,2]{1,2,3,0:T(8,128)S(1)}, u32[]{:S(2)}, u32[]{:S(2)}) collective-permute-start(f32[8,15,12,2]{1,2,3,0:T(8,128)S(1)} %get-tuple-element.152), channel_id=1, source_target_pairs={{4,0},{8,4},{12,8},{0,12},{5,1},{9,5},{13,9},{1,13},{6,2},{10,6},{... | collective-permute-start | bytes 34568 | tf_op jit(solution)/shard_map/ppermute | solution.py:31
  21.9 0.9 slice_bitcast_fusion.3
  22.8 1.7 %collective-permute-done.6 = f32[8,15,12,2]{1,2,3,0:T(8,128)S(1)} collective-permute-done((f32[8,15,12,2]{1,2,3,0:T(8,128)S(1)}, f32[8,15,12,2]{1,2,3,0:T(8,128)S(1)}, u32[]{:S(2)}, u32[]{:S(2)}) %collective-permute-start.6) | collective-permute-done | bytes 11552 | tf_op jit(solution)/shard_map/ppermute | solution.py:29
  25.6 0.8 subtract_multiply_fusion
  26.9 0.8 reshape.75
  27.6 4.7 %all-to-all-start.1 = ((f32[4,1,960]{2,1,0:T(1,128)}), f32[4,1,960]{2,1,0:T(1,128)S(1)}, u32[]{:S(2)}, u32[]{:S(2)}) async-start(f32[4,1,960]{2,1,0:T(1,128)} %reshape.75), calls=%async_computation.1 | async-start | bytes 32768 | tf_op jit(solution)/shard_map/all_to_all | solution.py:95
  32.3 1.2 pad_maximum_fusion
  33.5 2.3 %reshape.73 = f32[4,1,61440]{2,1,0:T(1,128)} reshape(f32[4,8,15,8,64]{4,3,2,1,0:T(8,128)S(1)} %pad_maximum_fusion) | data formatting | bytes 1966080
  35.8 2.2 %all-to-all-done.1 = f32[4,1,960]{2,1,0:T(1,128)S(1)} async-done(((f32[4,1,960]{2,1,0:T(1,128)}), f32[4,1,960]{2,1,0:T(1,128)S(1)}, u32[]{:S(2)}, u32[]{:S(2)}) %all-to-all-start.1) | async-done | bytes 15392 | tf_op jit(solution)/shard_map/all_to_all | solution.py:95
  38.0 3.7 %all-to-all-start = ((f32[4,1,61440]{2,1,0:T(1,128)}), f32[4,1,61440]{2,1,0:T(1,128)S(1)}, u32[]{:S(2)}, u32[]{:S(2)}) async-start(f32[4,1,61440]{2,1,0:T(1,128)} %reshape.73), calls=%async_computation | async-start | bytes 1966080 | tf_op jit(solution)/shard_map/all_to_all | solution.py:15
  42.1 0.6 broadcast.101
  42.7 0.7 reduce.1
  43.8 22.2 %all-to-all-done = f32[4,1,61440]{2,1,0:T(1,128)S(1)} async-done(((f32[4,1,61440]{2,1,0:T(1,128)}), f32[4,1,61440]{2,1,0:T(1,128)S(1)}, u32[]{:S(2)}, u32[]{:S(2)}) %all-to-all-start) | async-done | bytes 983072 | tf_op jit(solution)/shard_map/all_to_all | solution.py:15
  66.0 3.5 %reduce = f32[4,61440]{1,0:T(4,128)S(1)} reduce(f32[4,1,61440]{2,1,0:T(1,128)S(1)} %all-to-all-done, f32[]{:T(128)} %broadcast.101), dimensions={1}, to_apply=%all_to_all.27.reduce_sub_computation | reduce | bytes 1966084 | tf_op jit(solution)/shard_map/all_to_all | solution.py:15
  69.5 1.0 reshape.74
  70.6 1.1 copy.88
  71.9 53.0 %while.13 = (s32[]{:T(128)}, f32[8,60,8,64]{3,0,2,1:T(8,128)S(1)}, s32[8]{0:T(128)S(1)}, f32[8,60,8,1]{0,2,1,3:T(8,128)S(1)}, f32[8,8]{1,0:T(8,128)S(1)}, /*index=5*/s32[]{:T(128)}) while((s32[]{:T(128)}, f32[8,60,8,64]{3,0,2,1:T(8,128)S(1)}, s32[8]{0:T(128)S(1)}, f32[8,60,8,1]{0,2,1,3:T(8,128)S(1)}, f32[8,8]{1,0:T(8,128)S(1)}, ...), condition=%wide.region_1.2_spmd, body=%wide.region_0.1_spmd.sunk | while | flops 27525128 | bytes 15744385 | solution.py:65
  72.1 0.5 fusion.46
  72.6 0.8 fusion.45
  73.3 0.8 fusion.44
  74.1 4.4 %add_select_fusion.2 = f32[8,60,8,64]{3,0,2,1:T(8,128)S(1)} fusion(f32[8,60,8,64]{3,0,2,1:T(8,128)S(1)} %copy.130, f32[8,60,8,63]{3,0,2,1:T(8,128)S(1)} %get-tuple-element.198, f32[8,60,8,1]{3,0,2,1:T(8,128)S(1)} %get-tuple-element.199, f32[8,60,8,1]{3,0,2,1:T(8,128)S(1)} %get-tuple-element.200, f32[8,60,8,63]{3,0,2,1:T(8,128)S(1)} %get-tuple-element.201, ...), kind=kOutput, calls=%fused_computation.clone.1 | convolution fusion | flops 27525120 | bytes 5913864 | tf_op jit(solution)/shard_map/while/body/eval_jaxpr/gf,flsc->glsc/dot_general | solution.py:55
  79.2 0.8 fusion.45
  80.0 0.8 fusion.44
  80.8 4.4 %add_select_fusion.2 = f32[8,60,8,64]{3,0,2,1:T(8,128)S(1)} fusion(f32[8,60,8,64]{3,0,2,1:T(8,128)S(1)} %copy.130, f32[8,60,8,63]{3,0,2,1:T(8,128)S(1)} %get-tuple-element.198, f32[8,60,8,1]{3,0,2,1:T(8,128)S(1)} %get-tuple-element.199, f32[8,60,8,1]{3,0,2,1:T(8,128)S(1)} %get-tuple-element.200, f32[8,60,8,63]{3,0,2,1:T(8,128)S(1)} %get-tuple-element.201, ...), kind=kOutput, calls=%fused_computation.clone.1 | convolution fusion | flops 27525120 | bytes 5913864 | tf_op jit(solution)/shard_map/while/body/eval_jaxpr/gf,flsc->glsc/dot_general | solution.py:55
  85.3 0.5 fusion.46
  85.9 0.8 fusion.45
  86.6 0.8 fusion.44
  87.4 4.4 %add_select_fusion.2 = f32[8,60,8,64]{3,0,2,1:T(8,128)S(1)} fusion(f32[8,60,8,64]{3,0,2,1:T(8,128)S(1)} %copy.130, f32[8,60,8,63]{3,0,2,1:T(8,128)S(1)} %get-tuple-element.198, f32[8,60,8,1]{3,0,2,1:T(8,128)S(1)} %get-tuple-element.199, f32[8,60,8,1]{3,0,2,1:T(8,128)S(1)} %get-tuple-element.200, f32[8,60,8,63]{3,0,2,1:T(8,128)S(1)} %get-tuple-element.201, ...), kind=kOutput, calls=%fused_computation.clone.1 | convolution fusion | flops 27525120 | bytes 5913864 | tf_op jit(solution)/shard_map/while/body/eval_jaxpr/gf,flsc->glsc/dot_general | solution.py:55
  92.5 0.8 fusion.45
  93.3 0.8 fusion.44
  94.0 4.4 %add_select_fusion.2 = f32[8,60,8,64]{3,0,2,1:T(8,128)S(1)} fusion(f32[8,60,8,64]{3,0,2,1:T(8,128)S(1)} %copy.130, f32[8,60,8,63]{3,0,2,1:T(8,128)S(1)} %get-tuple-element.198, f32[8,60,8,1]{3,0,2,1:T(8,128)S(1)} %get-tuple-element.199, f32[8,60,8,1]{3,0,2,1:T(8,128)S(1)} %get-tuple-element.200, f32[8,60,8,63]{3,0,2,1:T(8,128)S(1)} %get-tuple-element.201, ...), kind=kOutput, calls=%fused_computation.clone.1 | convolution fusion | flops 27525120 | bytes 5913864 | tf_op jit(solution)/shard_map/while/body/eval_jaxpr/gf,flsc->glsc/dot_general | solution.py:55
  99.1 0.8 fusion.45
  99.9 0.8 fusion.44
  100.7 4.4 %add_select_fusion.2 = f32[8,60,8,64]{3,0,2,1:T(8,128)S(1)} fusion(f32[8,60,8,64]{3,0,2,1:T(8,128)S(1)} %copy.130, f32[8,60,8,63]{3,0,2,1:T(8,128)S(1)} %get-tuple-element.198, f32[8,60,8,1]{3,0,2,1:T(8,128)S(1)} %get-tuple-element.199, f32[8,60,8,1]{3,0,2,1:T(8,128)S(1)} %get-tuple-element.200, f32[8,60,8,63]{3,0,2,1:T(8,128)S(1)} %get-tuple-element.201, ...), kind=kOutput, calls=%fused_computation.clone.1 | convolution fusion | flops 27525120 | bytes 5913864 | tf_op jit(solution)/shard_map/while/body/eval_jaxpr/gf,flsc->glsc/dot_general | solution.py:55
  105.7 0.8 fusion.45
  106.5 0.8 fusion.44
  107.3 4.4 %add_select_fusion.2 = f32[8,60,8,64]{3,0,2,1:T(8,128)S(1)} fusion(f32[8,60,8,64]{3,0,2,1:T(8,128)S(1)} %copy.130, f32[8,60,8,63]{3,0,2,1:T(8,128)S(1)} %get-tuple-element.198, f32[8,60,8,1]{3,0,2,1:T(8,128)S(1)} %get-tuple-element.199, f32[8,60,8,1]{3,0,2,1:T(8,128)S(1)} %get-tuple-element.200, f32[8,60,8,63]{3,0,2,1:T(8,128)S(1)} %get-tuple-element.201, ...), kind=kOutput, calls=%fused_computation.clone.1 | convolution fusion | flops 27525120 | bytes 5913864 | tf_op jit(solution)/shard_map/while/body/eval_jaxpr/gf,flsc->glsc/dot_general | solution.py:55
  112.4 0.8 fusion.45
  113.1 0.8 fusion.44
  113.9 4.4 %add_select_fusion.2 = f32[8,60,8,64]{3,0,2,1:T(8,128)S(1)} fusion(f32[8,60,8,64]{3,0,2,1:T(8,128)S(1)} %copy.130, f32[8,60,8,63]{3,0,2,1:T(8,128)S(1)} %get-tuple-element.198, f32[8,60,8,1]{3,0,2,1:T(8,128)S(1)} %get-tuple-element.199, f32[8,60,8,1]{3,0,2,1:T(8,128)S(1)} %get-tuple-element.200, f32[8,60,8,63]{3,0,2,1:T(8,128)S(1)} %get-tuple-element.201, ...), kind=kOutput, calls=%fused_computation.clone.1 | convolution fusion | flops 27525120 | bytes 5913864 | tf_op jit(solution)/shard_map/while/body/eval_jaxpr/gf,flsc->glsc/dot_general | solution.py:55
  119.0 0.8 fusion.45
  119.8 0.8 fusion.44
  120.6 4.4 %add_select_fusion.2 = f32[8,60,8,64]{3,0,2,1:T(8,128)S(1)} fusion(f32[8,60,8,64]{3,0,2,1:T(8,128)S(1)} %copy.130, f32[8,60,8,63]{3,0,2,1:T(8,128)S(1)} %get-tuple-element.198, f32[8,60,8,1]{3,0,2,1:T(8,128)S(1)} %get-tuple-element.199, f32[8,60,8,1]{3,0,2,1:T(8,128)S(1)} %get-tuple-element.200, f32[8,60,8,63]{3,0,2,1:T(8,128)S(1)} %get-tuple-element.201, ...), kind=kOutput, calls=%fused_computation.clone.1 | convolution fusion | flops 27525120 | bytes 5913864 | tf_op jit(solution)/shard_map/while/body/eval_jaxpr/gf,flsc->glsc/dot_general | solution.py:55
  125.0 2.2 %fusion.12 = f32[8,60,8]{2,1,0:T(8,128)S(1)} fusion(f32[8,60,8,64]{3,2,1,0:T(8,128)} %bitcast.67, f32[8,60,8,64]{3,0,2,1:T(8,128)S(1)} %get-tuple-element.96), kind=kLoop, calls=%fused_computation.16 | loop fusion | flops 487680 | bytes 1981440 | tf_op jit(solution)/shard_map/reduce_sum | solution.py:102
  127.5 0.8 reshape.77
  128.2 3.2 %all-to-all-start.2 = ((f32[4,1,960]{2,1,0:T(1,128)}), f32[4,1,960]{2,1,0:T(1,128)S(1)}, u32[]{:S(2)}, u32[]{:S(2)}) async-start(f32[4,1,960]{2,1,0:T(1,128)} %reshape.77), calls=%async_computation.2 | async-start | bytes 32768 | tf_op jit(solution)/shard_map/all_to_all | solution.py:103
  131.5 1.7 %copy.96 = f32[8,60,8,64]{3,2,0,1:T(8,128)} copy(f32[8,60,8,64]{3,0,2,1:T(8,128)S(1)} %get-tuple-element.96) | data formatting | bytes 1966080 | tf_op jit(solution)/shard_map/while | solution.py:65
  133.2 2.7 %reshape.64 = f32[8,60,512]{2,0,1:T(8,128)} reshape(f32[8,60,8,64]{3,2,0,1:T(8,128)} %copy.96) | data formatting | bytes 1966080 | tf_op jit(solution)/shard_map/reshape | solution.py:107
  135.9 1.2 all-to-all-done.2
  137.1 0.7 reduce.2
  138.4 0.7 copy.97
  (79 shorter events, 9.6 us)
Async XLA Ops:
  0.6 11.3 %copy-start.1 = (f32[8,15,8,256]{3,2,1,0:T(8,128)S(1)}, f32[8,15,8,256]{3,2,1,0:T(8,128)}, u32[]{:S(2)}) copy-start(f32[8,15,8,256]{3,2,1,0:T(8,128)} %param.8) | copy-start | bytes 2949124
  1.7 4.9 %collective-permute-start = (f32[8,15,2,4]{1,2,3,0:T(2,128)S(1)}, f32[8,15,2,4]{1,2,3,0:T(2,128)S(1)}, u32[]{:S(2)}, u32[]{:S(2)}) collective-permute-start(f32[8,15,2,4]{1,2,3,0:T(2,128)S(1)} %get-tuple-element.157), channel_id=1, source_target_pairs={{0,16},{16,0},{1,17},{17,1},{2,18},{18,2},{3,19},{19,3},{4,20},{20... | collective-permute-start | bytes 11528 | tf_op jit(solution)/shard_map/ppermute | solution.py:29
  4.7 3.9 %collective-permute-start.1 = (f32[8,15,2,4]{1,2,3,0:T(2,128)S(1)}, f32[8,15,2,4]{1,2,3,0:T(2,128)S(1)}, u32[]{:S(2)}, u32[]{:S(2)}) collective-permute-start(f32[8,15,2,4]{1,2,3,0:T(2,128)S(1)} %get-tuple-element.158), channel_id=1, source_target_pairs={{16,0},{0,16},{17,1},{1,17},{18,2},{2,18},{19,3},{3,19},{20,4},{4,... | collective-permute-start | bytes 11528 | tf_op jit(solution)/shard_map/ppermute | solution.py:31
  9.4 4.6 %collective-permute-start.2 = (f32[8,15,12,2]{1,2,3,0:T(8,128)}, f32[8,15,12,2]{1,2,3,0:T(8,128)S(1)}, u32[]{:S(2)}, u32[]{:S(2)}) collective-permute-start(f32[8,15,12,2]{1,2,3,0:T(8,128)} %get-tuple-element.153), channel_id=1, source_target_pairs={{0,4},{4,8},{8,12},{12,0},{1,5},{5,9},{9,13},{13,1},{2,6},{6,10},{... | collective-permute-start | bytes 34568 | tf_op jit(solution)/shard_map/ppermute | solution.py:29
  9.4 5.0 %collective-permute-start.3 = (f32[8,15,12,2]{1,2,3,0:T(8,128)S(1)}, f32[8,15,12,2]{1,2,3,0:T(8,128)S(1)}, u32[]{:S(2)}, u32[]{:S(2)}) collective-permute-start(f32[8,15,12,2]{1,2,3,0:T(8,128)S(1)} %get-tuple-element.154), channel_id=1, source_target_pairs={{4,0},{8,4},{12,8},{0,12},{5,1},{9,5},{13,9},{1,13},{6,2},{10,6},{... | collective-permute-start | bytes 34568 | tf_op jit(solution)/shard_map/ppermute | solution.py:31
  15.0 4.3 %collective-permute-start.4 = (f32[8,15,2,4]{1,2,3,0:T(2,128)S(1)}, f32[8,15,2,4]{1,2,3,0:T(2,128)S(1)}, u32[]{:S(2)}, u32[]{:S(2)}) collective-permute-start(f32[8,15,2,4]{1,2,3,0:T(2,128)S(1)} %get-tuple-element.155), channel_id=1, source_target_pairs={{0,16},{16,0},{1,17},{17,1},{2,18},{18,2},{3,19},{19,3},{4,20},{20... | collective-permute-start | bytes 11528 | tf_op jit(solution)/shard_map/ppermute | solution.py:29
  15.6 4.4 %collective-permute-start.5 = (f32[8,15,2,4]{1,2,3,0:T(2,128)S(1)}, f32[8,15,2,4]{1,2,3,0:T(2,128)S(1)}, u32[]{:S(2)}, u32[]{:S(2)}) collective-permute-start(f32[8,15,2,4]{1,2,3,0:T(2,128)S(1)} %get-tuple-element.156), channel_id=1, source_target_pairs={{16,0},{0,16},{17,1},{1,17},{18,2},{2,18},{19,3},{3,19},{20,4},{4,... | collective-permute-start | bytes 11528 | tf_op jit(solution)/shard_map/ppermute | solution.py:31
  20.1 4.4 %collective-permute-start.6 = (f32[8,15,12,2]{1,2,3,0:T(8,128)S(1)}, f32[8,15,12,2]{1,2,3,0:T(8,128)S(1)}, u32[]{:S(2)}, u32[]{:S(2)}) collective-permute-start(f32[8,15,12,2]{1,2,3,0:T(8,128)S(1)} %get-tuple-element.151), channel_id=1, source_target_pairs={{0,4},{4,8},{8,12},{12,0},{1,5},{5,9},{9,13},{13,1},{2,6},{6,10},{... | collective-permute-start | bytes 34568 | tf_op jit(solution)/shard_map/ppermute | solution.py:29
  20.3 4.8 %collective-permute-start.7 = (f32[8,15,12,2]{1,2,3,0:T(8,128)S(1)}, f32[8,15,12,2]{1,2,3,0:T(8,128)S(1)}, u32[]{:S(2)}, u32[]{:S(2)}) collective-permute-start(f32[8,15,12,2]{1,2,3,0:T(8,128)S(1)} %get-tuple-element.152), channel_id=1, source_target_pairs={{4,0},{8,4},{12,8},{0,12},{5,1},{9,5},{13,9},{1,13},{6,2},{10,6},{... | collective-permute-start | bytes 34568 | tf_op jit(solution)/shard_map/ppermute | solution.py:31
  22.8 2.7 %copy-start.3 = (f32[8,15,8,4]{1,3,2,0:T(4,128)S(1)}, f32[8,15,8,4]{1,3,2,0:T(4,128)}, u32[]{:S(2)}) copy-start(f32[8,15,8,4]{1,3,2,0:T(4,128)} %param.7) | copy-start | bytes 46084
  27.6 10.3 %all-to-all-start.1 = ((f32[4,1,960]{2,1,0:T(1,128)}), f32[4,1,960]{2,1,0:T(1,128)S(1)}, u32[]{:S(2)}, u32[]{:S(2)}) async-start(f32[4,1,960]{2,1,0:T(1,128)} %reshape.75), calls=%async_computation.1 | async-start | bytes 32768 | tf_op jit(solution)/shard_map/all_to_all | solution.py:95
  33.5 8.2 %copy-start.6 = (s32[8,4]{0,1:T(4,128)S(1)}, s32[8,4]{0,1:T(4,128)}, u32[]{:S(2)}) copy-start(s32[8,4]{0,1:T(4,128)} %param.10) | copy-start | bytes 388
  38.0 28.1 %all-to-all-start = ((f32[4,1,61440]{2,1,0:T(1,128)}), f32[4,1,61440]{2,1,0:T(1,128)S(1)}, u32[]{:S(2)}, u32[]{:S(2)}) async-start(f32[4,1,61440]{2,1,0:T(1,128)} %reshape.73), calls=%async_computation | async-start | bytes 1966080 | tf_op jit(solution)/shard_map/all_to_all | solution.py:15
  70.6 1.3 copy-start
  70.6 1.3 copy-start.4
  128.2 8.8 %all-to-all-start.2 = ((f32[4,1,960]{2,1,0:T(1,128)}), f32[4,1,960]{2,1,0:T(1,128)S(1)}, u32[]{:S(2)}, u32[]{:S(2)}) async-start(f32[4,1,960]{2,1,0:T(1,128)} %reshape.77), calls=%async_computation.2 | async-start | bytes 32768 | tf_op jit(solution)/shard_map/all_to_all | solution.py:103
  133.2 5.0 %copy-start.2 = (f32[8,15,8,4]{1,2,3,0:T(8,128)S(1)}, f32[8,15,8,4]{1,2,3,0:T(8,128)}, u32[]{:S(2)}) copy-start(f32[8,15,8,4]{1,2,3,0:T(8,128)} %get-tuple-element.138) | copy-start | bytes 46084
  133.2 5.0 %copy-start.5 = (s32[8,4]{0,1:T(4,128)S(1)}, s32[8,4]{0,1:T(4,128)}, u32[]{:S(2)}) copy-start(s32[8,4]{0,1:T(4,128)} %param.11) | copy-start | bytes 388
